TPU v7x, 256 devices: a whole 4x4x8 slice. The times are simulated.
256 devices in a mesh: lat: 4 (over x_lo, core), lon: 4 (over y), lev: 4 (over z_hi, x_hi), unit: 4 (over z_lo).
Axes of the slice: x: 4 (x_hi: 2, x_lo: 2; x = x_hi * 2 + x_lo), y: 4, z: 8 (z_hi: 2, z_lo: 4; z = z_hi * 4 + z_lo), core: 2. Of those that a mesh axis runs over, the one named last changes fastest.
Arguments:
- tracer: float32 [64, 512, 64, 128], P(('unit', 'lat'), 'lon', 'lev'), parts along dimension 0, may hold values from 0.5 to 2
- diffusivity: float32 [64, 512, 64, 128], P(('unit', 'lat'), 'lon', 'lev'), parts along dimension 0, may hold values from 0.03 to 0.15
- source: float32 [64, 512, 64, 128], P(('unit', 'lat'), 'lon', 'lev'), parts along dimension 0, may hold values from -0.2 to 0.2
Outputs:
- standardized: float32 [64, 512, 64, 128], P(('unit', 'lat'), 'lon', 'lev'), parts along dimension 0
- tracer_end: float32 [64, 512, 64, 128], P(('unit', 'lat'), 'lon', 'lev'), parts along dimension 0
There are 4 independent parts, one for each index of `unit`. A program takes and returns all parts, laid end to end along the dimension named above; each array names one. Nothing has to cross between parts.
All inputs are finite; a program needn't handle non-finite values.
Results may differ from a plain program's by a relative error of at most 0.00002.
Values sent between devices are 32-bit elements; how exact they have to be, the bound alone decides.
A program may use at most 128 MiB of HBM per device.

v0:
```python
import functools

import jax
import jax.numpy as jnp
from jax import lax
from jax.experimental import pallas as pl
from jax.experimental.pallas import tpu as pltpu
from jax.sharding import PartitionSpec as P

STEPS = 4
CHUNKS = 8
LAG = 2
MESH = pl.DeviceIdType.MESH
F32 = jnp.float32


def stencil_kernel(
    n_lat, n_lon, n_lev,
    t_hbm, d_hbm, s_hbm,
    end_hbm, stat_hbm,
    te, dv, sv, ksend, khalo, stats, parts, mr,
    load_sem, out_sem, lat_send, lat_recv, lon_send, lon_recv, lev_send, lev_recv,
    rs_send, rs_recv, ag_send, ag_recv,
):
    rows, ni, nk, lanes = t_hbm.shape
    ci = ni // CHUNKS
    lat, lon, lev = lax.axis_index("lat"), lax.axis_index("lon"), lax.axis_index("lev")
    lat_to = ({"lat": lax.rem(lat + 1, n_lat)}, {"lat": lax.rem(lat + n_lat - 1, n_lat)})
    lon_to = ({"lon": lax.rem(lon + 1, n_lon)}, {"lon": lax.rem(lon + n_lon - 1, n_lon)})
    lev_to = [{"lev": lax.rem(lev + d, n_lev)} for d in range(1, n_lev)]

    def inner(c):
        return pl.ds(pl.multiple_of(c * ci, ci), ci)

    def padded(c):
        return pl.ds(1 + c * ci, ci)

    def remote(src, dst, send, recv, to):
        return pltpu.make_async_remote_copy(
            src_ref=src, dst_ref=dst, send_sem=send, recv_sem=recv, device_id=to, device_id_type=MESH
        )

    def lat_copy(t, c, d, first=False):
        row = (rows - 1, 0)[d]
        src = t_hbm.at[row, inner(c)] if first else te.at[t, row + 1, padded(c)]
        return remote(src, te.at[t, (0, rows + 1)[d], padded(c)], lat_send.at[d], lat_recv.at[d, t, c], lat_to[d])

    def lon_copy(t, d, first=False):
        col = (ni - 1, 0)[d]
        src = t_hbm.at[:, col] if first else te.at[t, pl.ds(1, rows), col + 1]
        return remote(src, te.at[t, pl.ds(1, rows), (0, ni + 1)[d]], lon_send.at[d], lon_recv.at[d, t], lon_to[d])

    def lev_copy(t, c, d):
        return remote(
            ksend.at[t, d, :, inner(c)], khalo.at[t, d, :, inner(c)],
            lev_send.at[d], lev_recv.at[d, t, c], lev_to[(0, n_lev - 2)[d]],
        )

    def rs_copy(c, d):
        row = lax.rem(lev + d, n_lev)
        return remote(
            stats.at[row, :, inner(c)], parts.at[d - 1, :, inner(c)],
            rs_send.at[d - 1], rs_recv.at[d - 1, c], lev_to[d - 1],
        )

    def ag_copy(c, d, row):
        return remote(
            mr.at[row, :, inner(c)], mr.at[row, :, inner(c)],
            ag_send.at[d - 1], ag_recv.at[d - 1, c], lev_to[d - 1],
        )

    loads = [
        pltpu.make_async_copy(t_hbm, te.at[0, pl.ds(1, rows), pl.ds(1, ni)], load_sem.at[0]),
        pltpu.make_async_copy(d_hbm, dv, load_sem.at[1]),
        pltpu.make_async_copy(s_hbm, sv, load_sem.at[2]),
    ]
    for load in loads:
        load.start()

    barrier = pltpu.get_barrier_semaphore()
    peers = [*lat_to, *lon_to, *lev_to]
    for peer in peers:
        pl.semaphore_signal(barrier, inc=1, device_id=peer, device_id_type=MESH)
    pl.semaphore_wait(barrier, len(peers))

    def first_lat(c, _):
        for d in (0, 1):
            lat_copy(0, c, d, True).start()
        return 0

    loads[0].wait()
    for d in (0, 1):
        lon_copy(0, d, True).start()

    def first_lev(c, _):
        def row(i, _):
            for j in range(rows):
                ksend[0, 0, j, pl.ds(i, 1), :] = te[0, j + 1, i + 1, pl.ds(nk - 1, 1), :]
                ksend[0, 1, j, pl.ds(i, 1), :] = te[0, j + 1, i + 1, pl.ds(0, 1), :]
            return 0

        lax.fori_loop(c * ci, (c + 1) * ci, row, 0)
        for d in (0, 1):
            lev_copy(0, c, d).start()
            lat_copy(0, c, d, True).start()
        return 0

    lax.fori_loop(0, CHUNKS, first_lev, 0)
    loads[1].wait()
    loads[2].wait()

    k_of = lax.broadcasted_iota(jnp.int32, (nk, lanes), 0)
    bottom, top = k_of == 0, k_of == nk - 1

    def update(t, c, last):
        def column(i, _):
            line = [te[t, j, i + 1] for j in range(rows + 2)]
            for j in range(rows):
                middle = line[j + 1]
                low = khalo[t, 0, j, pl.ds(i, 1), :]
                high = khalo[t, 1, j, pl.ds(i, 1), :]
                below = jnp.where(bottom, jnp.broadcast_to(low, middle.shape), pltpu.roll(middle, 1, 0))
                above = jnp.where(top, jnp.broadcast_to(high, middle.shape), pltpu.roll(middle, nk - 1, 0))
                spread = (
                    line[j] + line[j + 2] + te[t, j + 1, i] + te[t, j + 1, i + 2] + below + above - 6.0 * middle
                )
                new = middle + dv[j, i] * spread + sv[j, i]
                te[t + 1, j + 1, i + 1] = new
                if last:
                    total = jnp.sum(new, axis=0, keepdims=True)
                    off = new - total * (1.0 / nk)
                    stats[j, 0, pl.ds(i, 1), :] = total
                    stats[j, 1, pl.ds(i, 1), :] = jnp.sum(off * off, axis=0, keepdims=True)
                else:
                    ksend[t + 1, 0, j, pl.ds(i, 1), :] = new[nk - 1 :]
                    ksend[t + 1, 1, j, pl.ds(i, 1), :] = new[:1]
            return 0

        lax.fori_loop(c * ci, (c + 1) * ci, column, 0)

    def arrive(t, c):
        for d in (0, 1):
            lat_copy(t, c, d).wait_recv()
            lev_copy(t, c, d).wait_recv()

        @pl.when(c == 0)
        def _():
            lon_copy(t, 0).wait_recv()

        @pl.when(c == CHUNKS - 1)
        def _():
            lon_copy(t, 1).wait_recv()

    def step(t, _):
        def position(p, _):
            c = lax.rem(p + t + 1, CHUNKS)
            arrive(t, c)
            update(t, c, False)
            for d in (0, 1):
                lev_copy(t + 1, c, d).start()
                lat_copy(t + 1, c, d).start()

            @pl.when(c == CHUNKS - 1)
            def _():
                lon_copy(t + 1, 0).start()

            @pl.when(c == 0)
            def _():
                lon_copy(t + 1, 1).start()

            return 0

        return lax.fori_loop(0, CHUNKS, position, 0)

    lax.fori_loop(0, STEPS - 1, step, 0)

    final = STEPS - 1
    count = nk * n_lev

    def end_copy(c):
        return pltpu.make_async_copy(
            te.at[STEPS, pl.ds(1, rows), padded(c)], end_hbm.at[:, inner(c)], out_sem.at[c]
        )

    def chunk_at(p):
        return lax.rem(p + final + 1, CHUNKS)

    def reduce(p):
        c = chunk_at(p)
        for d in range(1, n_lev):
            rs_copy(c, d).wait_recv()
        totals = [stats[lev, 0, inner(c)], *(parts[d, 0, inner(c)] for d in range(n_lev - 1))]
        squares = [stats[lev, 1, inner(c)], *(parts[d, 1, inner(c)] for d in range(n_lev - 1))]
        mean = sum(totals[1:], totals[0]) * (1.0 / count)
        square = sum(squares[1:], squares[0])
        for total in totals:
            gap = total * (1.0 / nk) - mean
            square = square + nk * (gap * gap)
        mr[lev, 0, inner(c)] = mean
        mr[lev, 1, inner(c)] = lax.rsqrt(square * (1.0 / count) + 0.0001)
        for d in range(1, n_lev):
            ag_copy(c, d, lev).start()

    def last_position(p, _):
        c = chunk_at(p)
        arrive(final, c)
        update(final, c, True)
        for d in range(1, n_lev):
            rs_copy(c, d).start()
        end_copy(c).start()

        @pl.when(p >= LAG)
        def _():
            reduce(p - LAG)

        return 0

    lax.fori_loop(0, CHUNKS, last_position, 0)

    def drain(p, _):
        reduce(p)
        return 0

    lax.fori_loop(CHUNKS - LAG, CHUNKS, drain, 0)

    def finish(c, _):
        end_copy(c).wait()
        for d in range(1, n_lev):
            ag_copy(c, d, lax.rem(lev + n_lev - d, n_lev)).wait_recv()
        return 0

    lax.fori_loop(0, CHUNKS, finish, 0)
    out = pltpu.make_async_copy(mr, stat_hbm, load_sem.at[0])
    out.start()

    for d in (0, 1):
        pltpu.make_async_copy(dv, dv, lat_send.at[d]).wait()
        pltpu.make_async_copy(ksend.at[:, d], khalo.at[:, d], lev_send.at[d]).wait()
        whole = te.at[pl.ds(0, STEPS), pl.ds(1, rows), 0]
        pltpu.make_async_copy(whole, whole, lon_send.at[d]).wait()
    for d in range(n_lev - 1):
        pltpu.make_async_copy(parts.at[d], parts.at[d], rs_send.at[d]).wait()
        pltpu.make_async_copy(parts.at[d], parts.at[d], ag_send.at[d]).wait()
    out.wait()


def scale_kernel(t_ref, m_ref, o_ref, e_ref):
    value = t_ref[...]
    e_ref[...] = value
    o_ref[...] = (value - m_ref[:, 0][:, :, None, :]) * m_ref[:, 1][:, :, None, :]


def on_device(sizes, tracer, diffusivity, source):
    rows, ni, nk, lanes = tracer.shape
    n_lat, n_lon, n_lev = sizes
    any_space = pl.BlockSpec(memory_space=pl.ANY)
    dma, vmem = pltpu.SemaphoreType.DMA, pltpu.VMEM
    end, stat = pl.pallas_call(
        functools.partial(stencil_kernel, n_lat, n_lon, n_lev),
        out_shape=(
            jax.ShapeDtypeStruct(tracer.shape, F32),
            jax.ShapeDtypeStruct((rows, 2, ni, lanes), F32),
        ),
        in_specs=[any_space] * 3,
        out_specs=(any_space, any_space),
        scratch_shapes=[
            vmem((STEPS + 1, rows + 2, ni + 2, nk, lanes), F32),
            vmem((rows, ni, nk, lanes), F32),
            vmem((rows, ni, nk, lanes), F32),
            vmem((STEPS, 2, rows, ni, lanes), F32),
            vmem((STEPS, 2, rows, ni, lanes), F32),
            vmem((rows, 2, ni, lanes), F32),
            vmem((n_lev - 1, 2, ni, lanes), F32),
            vmem((rows, 2, ni, lanes), F32),
            dma((3,)), dma((CHUNKS,)),
            dma((2,)), dma((2, STEPS, CHUNKS)),
            dma((2,)), dma((2, STEPS)),
            dma((2,)), dma((2, STEPS, CHUNKS)),
            dma((n_lev - 1,)), dma((n_lev - 1, CHUNKS)),
            dma((n_lev - 1,)), dma((n_lev - 1, CHUNKS)),
        ],
        compiler_params=pltpu.CompilerParams(
            collective_id=0, has_side_effects=True, vmem_limit_bytes=60 * 2**20
        ),
        name="stencil",
    )(tracer, diffusivity, source)
    block = 32
    spec = pl.BlockSpec((1, block, nk, lanes), lambda j, i: (j, i, 0, 0))
    return pl.pallas_call(
        scale_kernel,
        grid=(rows, ni // block),
        out_shape=(jax.ShapeDtypeStruct(tracer.shape, F32), jax.ShapeDtypeStruct(tracer.shape, F32)),
        in_specs=[spec, pl.BlockSpec((1, 2, block, lanes), lambda j, i: (j, 0, i, 0))],
        out_specs=(spec, spec),
        name="scale",
    )(end, stat)


def solution(mesh):
    sizes = (mesh.shape["lat"], mesh.shape["lon"], mesh.shape["lev"])
    spec = P(("unit", "lat"), "lon", "lev", None)
    return jax.shard_map(
        functools.partial(on_device, sizes),
        mesh=mesh,
        in_specs=(spec, spec, spec),
        out_specs=(spec, spec),
        check_vma=False,
    )
```

profile of v0, /device:TPU:56, one launch (start us, length us, event | category | flops | bytes accessed | tf_op | source)
XLA Modules:
  0.0 187.2 jit_solution(16917982626077943402)
XLA Ops:
  0.6 175.8 %stencil.1 = (f32[4,128,16,128]{3,2,1,0:T(8,128)}, f32[4,2,128,128]{3,2,1,0:T(8,128)}) custom-call(f32[4,128,16,128]{3,2,1,0:T(8,128)} %t_hbm.1, f32[4,128,16,128]{3,2,1,0:T(8,128)} %d_hbm.1, f32[4,128,16,128]{3,2,1,0:T(8,128)} %s_hbm.1), custom_call_target="tpu_custom_call" | custom-call | tf_op jit(solution)/shard_map/stencil/pallas_call | solution.py:258
  176.5 10.8 %scale.1 = (f32[4,128,16,128]{3,2,1,0:T(8,128)}, f32[4,128,16,128]{3,2,1,0:T(8,128)}) custom-call(f32[4,128,16,128]{3,2,1,0:T(8,128)} %get-tuple-element.4.t_ref, f32[4,2,128,128]{3,2,1,0:T(8,128)} %get-tuple-element.5.m_ref), custom_call_target="tpu_custom_call" | custom-call | tf_op jit(solution)/shard_map/scale/pallas_call | solution.py:289
where the time goes:
time: 188 us; the launch traced here: 187 us
  Pallas kernels  187 us (99%)
    pallas_call x1, Pallas kernels, on_device(): pl.pallas_call(functools.partial(stencil_kernel, n_lat, n_lon, n_lev), ou...  176 us
    pallas_call x1, Pallas kernels, on_device(): pl.pallas_call(scale_kernel, grid=(rows, ni // block), out_shape=(jax.Sha...  10.8 us

commit v1 on v0

v1 whole, which is shorter than its diff:
```python
import functools

import jax
import jax.numpy as jnp
from jax import lax
from jax.experimental import pallas as pl
from jax.experimental.pallas import tpu as pltpu
from jax.sharding import PartitionSpec as P

STEPS = 4
CHUNKS = 8
END_LAG = 4
PAIR_LAG = END_LAG + 2
FAR_LAG = PAIR_LAG + 3
MESH = pl.DeviceIdType.MESH
F32 = jnp.float32


def stencil_kernel(
    n_lat, n_lon, n_lev,
    t_hbm, d_hbm, s_hbm,
    end_ref, stat_ref,
    te, dv, sv, ksend, khalo, stats, parts, paired, far, mr,
    load_sem, lat_send, lat_recv, lon_send, lon_recv, lev_send, lev_recv,
    rs_send, rs_recv, far_send, far_recv, ag_send, ag_recv,
):
    rows, ni, nk, lanes = t_hbm.shape
    ci = ni // CHUNKS
    lat, lon, lev = lax.axis_index("lat"), lax.axis_index("lon"), lax.axis_index("lev")
    lat_to = ({"lat": lax.rem(lat + 1, n_lat)}, {"lat": lax.rem(lat + n_lat - 1, n_lat)})
    lon_to = ({"lon": lax.rem(lon + 1, n_lon)}, {"lon": lax.rem(lon + n_lon - 1, n_lon)})
    lev_to = [{"lev": lax.rem(lev + d, n_lev)} for d in range(1, n_lev)]

    def inner(c):
        return pl.ds(pl.multiple_of(c * ci, ci), ci)

    def padded(c):
        return pl.ds(1 + c * ci, ci)

    def remote(src, dst, send, recv, to):
        return pltpu.make_async_remote_copy(
            src_ref=src, dst_ref=dst, send_sem=send, recv_sem=recv, device_id=to, device_id_type=MESH
        )

    def lat_copy(t, c, d, first=False):
        row = (rows - 1, 0)[d]
        src = t_hbm.at[row, inner(c)] if first else te.at[t, row + 1, padded(c)]
        return remote(src, te.at[t, (0, rows + 1)[d], padded(c)], lat_send.at[d], lat_recv.at[d, t, c], lat_to[d])

    def lon_copy(t, d, first=False):
        col = (ni - 1, 0)[d]
        src = t_hbm.at[:, col] if first else te.at[t, pl.ds(1, rows), col + 1]
        return remote(src, te.at[t, pl.ds(1, rows), (0, ni + 1)[d]], lon_send.at[d], lon_recv.at[d, t], lon_to[d])

    def lev_copy(t, c, d):
        return remote(
            ksend.at[t, d, :, inner(c)], khalo.at[t, d, :, inner(c)],
            lev_send.at[d], lev_recv.at[d, t, c], lev_to[(0, n_lev - 2)[d]],
        )

    half = rows // 2
    side = lax.rem(lev, 2)
    mine, other = pl.ds(half * side, half), pl.ds(half * (1 - side), half)
    pair_to = {"lev": lev + 1 - 2 * side}
    far_to = lev_to[1]

    def rs_copy(c):
        return remote(stats.at[other, :, inner(c)], parts.at[:, :, inner(c)], rs_send.at[0], rs_recv.at[c], pair_to)

    def far_copy(c):
        return remote(paired.at[:, :, inner(c)], far.at[:, :, inner(c)], far_send.at[0], far_recv.at[c], far_to)

    def ag_copy(c, which):
        return remote(mr.at[which, :, inner(c)], mr.at[which, :, inner(c)], ag_send.at[0], ag_recv.at[c], pair_to)

    loads = [
        pltpu.make_async_copy(t_hbm, te.at[0, pl.ds(1, rows), pl.ds(1, ni)], load_sem.at[0]),
        pltpu.make_async_copy(d_hbm, dv, load_sem.at[1]),
        pltpu.make_async_copy(s_hbm, sv, load_sem.at[2]),
    ]
    for load in loads:
        load.start()

    barrier = pltpu.get_barrier_semaphore()
    peers = [*lat_to, *lon_to, *lev_to]
    for peer in peers:
        pl.semaphore_signal(barrier, inc=1, device_id=peer, device_id_type=MESH)
    pl.semaphore_wait(barrier, len(peers))

    loads[0].wait()
    for d in (0, 1):
        lon_copy(0, d, True).start()

    def first_lev(c, _):
        def row(i, _):
            for j in range(rows):
                ksend[0, 0, j, pl.ds(i, 1), :] = te[0, j + 1, i + 1, pl.ds(nk - 1, 1), :]
                ksend[0, 1, j, pl.ds(i, 1), :] = te[0, j + 1, i + 1, pl.ds(0, 1), :]
            return 0

        lax.fori_loop(c * ci, (c + 1) * ci, row, 0)
        for d in (0, 1):
            lev_copy(0, c, d).start()
            lat_copy(0, c, d, True).start()
        return 0

    lax.fori_loop(0, CHUNKS, first_lev, 0)
    loads[1].wait()
    loads[2].wait()

    k_of = lax.broadcasted_iota(jnp.int32, (nk, lanes), 0)
    bottom, top = k_of == 0, k_of == nk - 1

    def update(t, c, last):
        def column(i, _):
            line = [te[t, j, i + 1] for j in range(rows + 2)]
            for j in range(rows):
                middle = line[j + 1]
                low = khalo[t, 0, j, pl.ds(i, 1), :]
                high = khalo[t, 1, j, pl.ds(i, 1), :]
                below = jnp.where(bottom, jnp.broadcast_to(low, middle.shape), pltpu.roll(middle, 1, 0))
                above = jnp.where(top, jnp.broadcast_to(high, middle.shape), pltpu.roll(middle, nk - 1, 0))
                spread = (
                    line[j] + line[j + 2] + te[t, j + 1, i] + te[t, j + 1, i + 2] + below + above - 6.0 * middle
                )
                new = middle + dv[j, i] * spread + sv[j, i]
                if last:
                    end_ref[j, i] = new
                    total = jnp.sum(new, axis=0, keepdims=True)
                    off = new - total * (1.0 / nk)
                    stats[j, 0, pl.ds(i, 1), :] = total
                    stats[j, 1, pl.ds(i, 1), :] = jnp.sum(off * off, axis=0, keepdims=True)
                else:
                    te[t + 1, j + 1, i + 1] = new
                    ksend[t + 1, 0, j, pl.ds(i, 1), :] = new[nk - 1 :]
                    ksend[t + 1, 1, j, pl.ds(i, 1), :] = new[:1]
            return 0

        lax.fori_loop(c * ci, (c + 1) * ci, column, 0)

    def arrive(t, c):
        for d in (0, 1):
            lat_copy(t, c, d).wait_recv()
            lev_copy(t, c, d).wait_recv()

        @pl.when(c == 0)
        def _():
            lon_copy(t, 0).wait_recv()

        @pl.when(c == CHUNKS - 1)
        def _():
            lon_copy(t, 1).wait_recv()

    def position(t, p):
        c = lax.rem(p + t + 1, CHUNKS)
        arrive(t, c)
        update(t, c, False)
        for d in (0, 1):
            lev_copy(t + 1, c, d).start()
            lat_copy(t + 1, c, d).start()

        @pl.when(c == CHUNKS - 1)
        def _():
            lon_copy(t + 1, 0).start()

        @pl.when(c == 0)
        def _():
            lon_copy(t + 1, 1).start()

    def step(g, _):
        position(lax.div(g, CHUNKS), lax.rem(g, CHUNKS))
        return 0

    lax.fori_loop(0, (STEPS - 2) * CHUNKS, step, 0)

    final = STEPS - 1
    count = nk * n_lev

    def chunk_at(p):
        return lax.rem(p + final + 1, CHUNKS)

    def joined(total_a, square_a, total_b, square_b, cells):
        gap = (total_a - total_b) * (1.0 / cells)
        return total_a + total_b, square_a + square_b + (0.5 * cells) * (gap * gap)

    def pair_up(p):
        c = chunk_at(p)
        rs_copy(c).wait_recv()
        for r in range(half):
            row = half * side + r
            total, square = joined(
                stats[row, 0, inner(c)], stats[row, 1, inner(c)], parts[r, 0, inner(c)], parts[r, 1, inner(c)], nk
            )
            paired[r, 0, inner(c)] = total
            paired[r, 1, inner(c)] = square
        far_copy(c).start()

    def reduce(p):
        c = chunk_at(p)
        far_copy(c).wait_recv()
        for r in range(half):
            row = half * side + r
            total, square = joined(
                paired[r, 0, inner(c)], paired[r, 1, inner(c)], far[r, 0, inner(c)], far[r, 1, inner(c)], 2 * nk
            )
            mr[row, 0, inner(c)] = total * (1.0 / count)
            mr[row, 1, inner(c)] = lax.rsqrt(square * (1.0 / count) + 0.0001)
        ag_copy(c, mine).start()

    def last_position(p, _):
        @pl.when(p < CHUNKS)
        def _():
            position(final - 1, p)

        @pl.when((p >= END_LAG) & (p < CHUNKS + END_LAG))
        def _():
            c = chunk_at(p - END_LAG)
            arrive(final, c)
            update(final, c, True)
            rs_copy(c).start()

        @pl.when((p >= PAIR_LAG) & (p < CHUNKS + PAIR_LAG))
        def _():
            pair_up(p - PAIR_LAG)

        @pl.when(p >= FAR_LAG)
        def _():
            reduce(p - FAR_LAG)

        return 0

    lax.fori_loop(0, CHUNKS + FAR_LAG, last_position, 0)

    def finish(c, _):
        ag_copy(c, other).wait_recv()
        return 0

    lax.fori_loop(0, CHUNKS, finish, 0)
    stat_ref[...] = mr[...]

    for d in (0, 1):
        pltpu.make_async_copy(dv, dv, lat_send.at[d]).wait()
        pltpu.make_async_copy(ksend.at[:, d], khalo.at[:, d], lev_send.at[d]).wait()
        whole = te.at[pl.ds(0, STEPS), pl.ds(1, rows), 0]
        pltpu.make_async_copy(whole, whole, lon_send.at[d]).wait()
    for sem in (rs_send, far_send, ag_send):
        pltpu.make_async_copy(parts, far, sem.at[0]).wait()


def scale_kernel(t_ref, m_ref, o_hbm, e_hbm, scaled, sems):
    rows, ni = t_ref.shape[:2]
    ends = pltpu.make_async_copy(t_ref, e_hbm, sems.at[rows])
    ends.start()
    for j in range(rows):

        def column(i, _):
            value = t_ref[j, i]
            mean = jnp.broadcast_to(m_ref[j, 0, pl.ds(i, 1), :], value.shape)
            scale = jnp.broadcast_to(m_ref[j, 1, pl.ds(i, 1), :], value.shape)
            scaled[j, i] = (value - mean) * scale
            return 0

        lax.fori_loop(0, ni, column, 0, unroll=8)
        pltpu.make_async_copy(scaled.at[j], o_hbm.at[j], sems.at[j]).start()
    for j in range(rows):
        pltpu.make_async_copy(scaled.at[j], o_hbm.at[j], sems.at[j]).wait()
    ends.wait()


def on_device(sizes, tracer, diffusivity, source):
    rows, ni, nk, lanes = tracer.shape
    n_lat, n_lon, n_lev = sizes
    any_space = pl.BlockSpec(memory_space=pl.ANY)
    in_vmem = pl.BlockSpec(memory_space=pltpu.VMEM)
    dma, vmem = pltpu.SemaphoreType.DMA, pltpu.VMEM
    end, stat = pl.pallas_call(
        functools.partial(stencil_kernel, n_lat, n_lon, n_lev),
        out_shape=(vmem(tracer.shape, F32), vmem((rows, 2, ni, lanes), F32)),
        in_specs=[any_space] * 3,
        out_specs=(in_vmem, in_vmem),
        scratch_shapes=[
            vmem((STEPS, rows + 2, ni + 2, nk, lanes), F32),
            vmem((rows, ni, nk, lanes), F32),
            vmem((rows, ni, nk, lanes), F32),
            vmem((STEPS, 2, rows, ni, lanes), F32),
            vmem((STEPS, 2, rows, ni, lanes), F32),
            vmem((rows, 2, ni, lanes), F32),
            vmem((rows // 2, 2, ni, lanes), F32),
            vmem((rows // 2, 2, ni, lanes), F32),
            vmem((rows // 2, 2, ni, lanes), F32),
            vmem((rows, 2, ni, lanes), F32),
            dma((3,)),
            dma((2,)), dma((2, STEPS, CHUNKS)),
            dma((2,)), dma((2, STEPS)),
            dma((2,)), dma((2, STEPS, CHUNKS)),
            dma((1,)), dma((CHUNKS,)),
            dma((1,)), dma((CHUNKS,)),
            dma((1,)), dma((CHUNKS,)),
        ],
        compiler_params=pltpu.CompilerParams(
            collective_id=0, has_side_effects=True, vmem_limit_bytes=48 * 2**20
        ),
        name="stencil",
    )(tracer, diffusivity, source)
    whole = jax.ShapeDtypeStruct(tracer.shape, F32)
    return pl.pallas_call(
        scale_kernel,
        out_shape=(whole, whole),
        in_specs=[in_vmem, in_vmem],
        out_specs=(any_space, any_space),
        scratch_shapes=[vmem(tracer.shape, F32), dma((rows + 1,))],
        compiler_params=pltpu.CompilerParams(vmem_limit_bytes=6 * 2**20),
        name="scale",
    )(end, stat)


def solution(mesh):
    sizes = (mesh.shape["lat"], mesh.shape["lon"], mesh.shape["lev"])
    spec = P(("unit", "lat"), "lon", "lev", None)
    return jax.shard_map(
        functools.partial(on_device, sizes),
        mesh=mesh,
        in_specs=(spec, spec, spec),
        out_specs=(spec, spec),
        check_vma=False,
    )
```

time: 188 us -> 170 us (0.904)
  Pallas kernels: 187 us -> 168 us
    pallas_call x1, Pallas kernels: 176 us -> 164 us  [on_device(): pl.pallas_call(functools.partial(stencil_kernel, n_lat, n_lon, n_lev), ou...]
    pallas_call x1, Pallas kernels: 10.8 us -> 3.34 us  [on_device(): pl.pallas_call(scale_kernel, out_shape=(whole, whole), in_specs=[in_vmem,...]
where the time goes in v1:
time: 170 us; the launch traced here: 168 us
  Pallas kernels  168 us (99%)
    pallas_call x1, Pallas kernels, on_device(): pl.pallas_call(functools.partial(stencil_kernel, n_lat, n_lon, n_lev), ou...  164 us

profile of v1, /device:TPU:56, one launch (start us, length us, event | category | flops | bytes accessed | tf_op | source)
XLA Modules:
  0.0 168.5 jit_solution(43990053615533796)
XLA Ops:
  0.6 164.5 %stencil.1 = (f32[4,128,16,128]{3,2,1,0:T(8,128)S(1)}, f32[4,2,128,128]{3,2,1,0:T(8,128)S(1)}) custom-call(f32[4,128,16,128]{3,2,1,0:T(8,128)} %t_hbm.1, f32[4,128,16,128]{3,2,1,0:T(8,128)} %d_hbm.1, f32[4,128,16,128]{3,2,1,0:T(8,128)} %s_hbm.1), custom_call_target="tpu_custom_call" | custom-call | tf_op jit(solution)/shard_map/stencil/pallas_call | solution.py:276
  165.1 3.3 %scale.1 = (f32[4,128,16,128]{3,2,1,0:T(8,128)}, f32[4,128,16,128]{3,2,1,0:T(8,128)}) custom-call(f32[4,128,16,128]{3,2,1,0:T(8,128)S(1)} %get-tuple-element.4.t_ref, f32[4,2,128,128]{3,2,1,0:T(8,128)S(1)} %get-tuple-element.5.m_ref), custom_call_target="tpu_custom_call" | custom-call | tf_op jit(solution)/shard_map/scale/pallas_call | solution.py:306

commit v2 on v1

--- a/solution.py
+++ b/solution.py
@@ -9,7 +9,10 @@
 
 STEPS = 4
 CHUNKS = 8
-END_LAG = 4
+EAGER = 2
+AHEAD = 2
+END_AHEAD = 2
+END_LAG = 5
 PAIR_LAG = END_LAG + 2
 FAR_LAG = PAIR_LAG + 3
 MESH = pl.DeviceIdType.MESH
@@ -20,8 +23,8 @@
     n_lat, n_lon, n_lev,
     t_hbm, d_hbm, s_hbm,
     end_ref, stat_ref,
-    te, dv, sv, ksend, khalo, stats, parts, paired, far, mr,
-    load_sem, lat_send, lat_recv, lon_send, lon_recv, lev_send, lev_recv,
+    te, dv, sv, ksend, khalo, kon, stats, parts, paired, far, mr,
+    load_sem, lat_send, lat_recv, lon_send, lon_recv, lev_send, lev_recv, on_send, on_recv,
     rs_send, rs_recv, far_send, far_recv, ag_send, ag_recv,
 ):
     rows, ni, nk, lanes = t_hbm.shape
@@ -52,11 +55,39 @@
         src = t_hbm.at[:, col] if first else te.at[t, pl.ds(1, rows), col + 1]
         return remote(src, te.at[t, pl.ds(1, rows), (0, ni + 1)[d]], lon_send.at[d], lon_recv.at[d, t], lon_to[d])
 
+    odd = lax.rem(lat, 2)
+    facing = lax.rem(lat + n_lat + 2 * odd - 1, n_lat)
+    sent_rows, my_row, its_row = pl.ds(1 - odd, rows - 1), (rows - 1) * odd, (rows - 1) * (1 - odd)
+    on_to = [{"lat": facing, "lev": lax.rem(lev + 1, n_lev)}, {"lat": facing, "lev": lax.rem(lev + n_lev - 1, n_lev)}]
+
     def lev_copy(t, c, d):
         return remote(
-            ksend.at[t, d, :, inner(c)], khalo.at[t, d, :, inner(c)],
+            ksend.at[t, d, sent_rows, inner(c)], khalo.at[t, d, sent_rows, inner(c)],
             lev_send.at[d], lev_recv.at[d, t, c], lev_to[(0, n_lev - 2)[d]],
         )
+
+    def on_copy(t, c, d, row):
+        return remote(
+            kon.at[t, d, inner(c)], khalo.at[t, d, row, inner(c)], on_send.at[d], on_recv.at[d, t, c], on_to[d]
+        )
+
+    def lat_wait(t, c, d):
+        halo = te.at[t, (rows + 1) * d, padded(c)]
+        remote(halo, halo, lat_send.at[d], lat_recv.at[d, t, c], lat_to[0]).wait_recv()
+
+    def hand_on(t, p):
+        c = lax.rem(p + t + 1, CHUNKS)
+        lat_wait(t, c, odd)
+        halo = (rows + 1) * odd
+
+        def row(i, _):
+            kon[t, 0, pl.ds(i, 1), :] = te[t, halo, i + 1, pl.ds(nk - 1, 1), :]
+            kon[t, 1, pl.ds(i, 1), :] = te[t, halo, i + 1, pl.ds(0, 1), :]
+            return 0
+
+        lax.fori_loop(c * ci, (c + 1) * ci, row, 0)
+        for d in (0, 1):
+            on_copy(t, c, d, its_row).start()
 
     half = rows // 2
     side = lax.rem(lev, 2)
@@ -78,18 +109,25 @@
         pltpu.make_async_copy(d_hbm, dv, load_sem.at[1]),
         pltpu.make_async_copy(s_hbm, sv, load_sem.at[2]),
     ]
-    for load in loads:
-        load.start()
+    loads[0].start()
 
     barrier = pltpu.get_barrier_semaphore()
-    peers = [*lat_to, *lon_to, *lev_to]
+    peers = [*lat_to, *lon_to, *lev_to, *on_to]
     for peer in peers:
         pl.semaphore_signal(barrier, inc=1, device_id=peer, device_id_type=MESH)
     pl.semaphore_wait(barrier, len(peers))
 
-    loads[0].wait()
+    def first_lat(c, _):
+        for d in (0, 1):
+            lat_copy(0, c, d, True).start()
+        return 0
+
+    lax.fori_loop(0, EAGER, first_lat, 0)
+    for load in loads[1:]:
+        load.start()
     for d in (0, 1):
         lon_copy(0, d, True).start()
+    loads[0].wait()
 
     def first_lev(c, _):
         def row(i, _):
@@ -101,7 +139,11 @@
         lax.fori_loop(c * ci, (c + 1) * ci, row, 0)
         for d in (0, 1):
             lev_copy(0, c, d).start()
-            lat_copy(0, c, d, True).start()
+
+        @pl.when(c + EAGER < CHUNKS)
+        def _():
+            first_lat(c + EAGER, 0)
+
         return 0
 
     lax.fori_loop(0, CHUNKS, first_lev, 0)
@@ -139,9 +181,10 @@
         lax.fori_loop(c * ci, (c + 1) * ci, column, 0)
 
     def arrive(t, c):
-        for d in (0, 1):
-            lat_copy(t, c, d).wait_recv()
+        lat_wait(t, c, 1 - odd)
+        for d in (0, 1):
             lev_copy(t, c, d).wait_recv()
+            on_copy(t, c, d, my_row).wait_recv()
 
         @pl.when(c == 0)
         def _():
@@ -168,9 +211,15 @@
             lon_copy(t + 1, 1).start()
 
     def step(g, _):
+        hand_on(lax.div(g + AHEAD, CHUNKS), lax.rem(g + AHEAD, CHUNKS))
         position(lax.div(g, CHUNKS), lax.rem(g, CHUNKS))
         return 0
 
+    def first_on(p, _):
+        hand_on(0, p)
+        return 0
+
+    lax.fori_loop(0, AHEAD, first_on, 0)
     lax.fori_loop(0, (STEPS - 2) * CHUNKS, step, 0)
 
     final = STEPS - 1
@@ -208,9 +257,17 @@
         ag_copy(c, mine).start()
 
     def last_position(p, _):
+        @pl.when(p < CHUNKS - AHEAD)
+        def _():
+            hand_on(final - 1, p + AHEAD)
+
         @pl.when(p < CHUNKS)
         def _():
             position(final - 1, p)
+
+        @pl.when((p >= END_LAG - END_AHEAD) & (p < CHUNKS + END_LAG - END_AHEAD))
+        def _():
+            hand_on(final, p - END_LAG + END_AHEAD)
 
         @pl.when((p >= END_LAG) & (p < CHUNKS + END_LAG))
         def _():
@@ -240,7 +297,9 @@
 
     for d in (0, 1):
         pltpu.make_async_copy(dv, dv, lat_send.at[d]).wait()
-        pltpu.make_async_copy(ksend.at[:, d], khalo.at[:, d], lev_send.at[d]).wait()
+        edges = ksend.at[:, d, pl.ds(0, rows - 1)]
+        pltpu.make_async_copy(edges, edges, lev_send.at[d]).wait()
+        pltpu.make_async_copy(kon.at[:, d], kon.at[:, d], on_send.at[d]).wait()
         whole = te.at[pl.ds(0, STEPS), pl.ds(1, rows), 0]
         pltpu.make_async_copy(whole, whole, lon_send.at[d]).wait()
     for sem in (rs_send, far_send, ag_send):
@@ -284,6 +343,7 @@
             vmem((rows, ni, nk, lanes), F32),
             vmem((STEPS, 2, rows, ni, lanes), F32),
             vmem((STEPS, 2, rows, ni, lanes), F32),
+            vmem((STEPS, 2, ni, lanes), F32),
             vmem((rows, 2, ni, lanes), F32),
             vmem((rows // 2, 2, ni, lanes), F32),
             vmem((rows // 2, 2, ni, lanes), F32),
@@ -292,6 +352,7 @@
             dma((3,)),
             dma((2,)), dma((2, STEPS, CHUNKS)),
             dma((2,)), dma((2, STEPS)),
+            dma((2,)), dma((2, STEPS, CHUNKS)),
             dma((2,)), dma((2, STEPS, CHUNKS)),
             dma((1,)), dma((CHUNKS,)),
             dma((1,)), dma((CHUNKS,)),

time: 170 us -> 163 us (0.959)
  Pallas kernels: 168 us -> 162 us
    pallas_call x1, Pallas kernels: 164 us -> 159 us  [on_device(): pl.pallas_call(functools.partial(stencil_kernel, n_lat, n_lon, n_lev), ou...]
where the time goes in v2:
time: 163 us
  Pallas kernels  162 us (99%)
    pallas_call x1, Pallas kernels, on_device(): pl.pallas_call(functools.partial(stencil_kernel, n_lat, n_lon, n_lev), ou...  159 us
    pallas_call x1, Pallas kernels, on_device(): pl.pallas_call(scale_kernel, out_shape=(whole, whole), in_specs=[in_vmem,...  3.34 us

profile of v2, /device:TPU:56, one launch (start us, length us, event | category | flops | bytes accessed | tf_op | source)
XLA Modules:
  0.0 162.7 jit_solution(6299391704304510040)
XLA Ops:
  0.6 158.8 %stencil.1 = (f32[4,128,16,128]{3,2,1,0:T(8,128)S(1)}, f32[4,2,128,128]{3,2,1,0:T(8,128)S(1)}) custom-call(f32[4,128,16,128]{3,2,1,0:T(8,128)} %t_hbm.1, f32[4,128,16,128]{3,2,1,0:T(8,128)} %d_hbm.1, f32[4,128,16,128]{3,2,1,0:T(8,128)} %s_hbm.1), custom_call_target="tpu_custom_call" | custom-call | tf_op jit(solution)/shard_map/stencil/pallas_call | solution.py:335
  159.4 3.3 %scale.1 = (f32[4,128,16,128]{3,2,1,0:T(8,128)}, f32[4,128,16,128]{3,2,1,0:T(8,128)}) custom-call(f32[4,128,16,128]{3,2,1,0:T(8,128)S(1)} %get-tuple-element.4.t_ref, f32[4,2,128,128]{3,2,1,0:T(8,128)S(1)} %get-tuple-element.5.m_ref), custom_call_target="tpu_custom_call" | custom-call | tf_op jit(solution)/shard_map/scale/pallas_call | solution.py:367

commit v3 on v2

--- a/solution.py
+++ b/solution.py
@@ -13,8 +13,8 @@
 AHEAD = 2
 END_AHEAD = 2
 END_LAG = 5
-PAIR_LAG = END_LAG + 2
-FAR_LAG = PAIR_LAG + 3
+PAIR_LAG = END_LAG + 3
+FAR_LAG = PAIR_LAG + 2
 MESH = pl.DeviceIdType.MESH
 F32 = jnp.float32
 
@@ -23,9 +23,9 @@
     n_lat, n_lon, n_lev,
     t_hbm, d_hbm, s_hbm,
     end_ref, stat_ref,
-    te, dv, sv, ksend, khalo, kon, stats, parts, paired, far, mr,
+    te, dv, sv, ksend, khalo, kon, stats, parts, paired, far,
     load_sem, lat_send, lat_recv, lon_send, lon_recv, lev_send, lev_recv, on_send, on_recv,
-    rs_send, rs_recv, far_send, far_recv, ag_send, ag_recv,
+    pair_send, pair_recv, far_send, far_recv,
 ):
     rows, ni, nk, lanes = t_hbm.shape
     ci = ni // CHUNKS
@@ -89,20 +89,13 @@
         for d in (0, 1):
             on_copy(t, c, d, its_row).start()
 
-    half = rows // 2
-    side = lax.rem(lev, 2)
-    mine, other = pl.ds(half * side, half), pl.ds(half * (1 - side), half)
-    pair_to = {"lev": lev + 1 - 2 * side}
-    far_to = lev_to[1]
-
-    def rs_copy(c):
-        return remote(stats.at[other, :, inner(c)], parts.at[:, :, inner(c)], rs_send.at[0], rs_recv.at[c], pair_to)
-
-    def far_copy(c):
-        return remote(paired.at[:, :, inner(c)], far.at[:, :, inner(c)], far_send.at[0], far_recv.at[c], far_to)
-
-    def ag_copy(c, which):
-        return remote(mr.at[which, :, inner(c)], mr.at[which, :, inner(c)], ag_send.at[0], ag_recv.at[c], pair_to)
+    pair_to, far_to = {"lev": lev + 1 - 2 * lax.rem(lev, 2)}, lev_to[1]
+
+    def first_copy(c):
+        return remote(stats.at[:, :, inner(c)], parts.at[:, :, inner(c)], pair_send.at[0], pair_recv.at[c], far_to)
+
+    def second_copy(c):
+        return remote(paired.at[:, :, inner(c)], far.at[:, :, inner(c)], far_send.at[0], far_recv.at[c], pair_to)
 
     loads = [
         pltpu.make_async_copy(t_hbm, te.at[0, pl.ds(1, rows), pl.ds(1, ni)], load_sem.at[0]),
@@ -234,27 +227,24 @@
 
     def pair_up(p):
         c = chunk_at(p)
-        rs_copy(c).wait_recv()
-        for r in range(half):
-            row = half * side + r
+        first_copy(c).wait_recv()
+        for r in range(rows):
             total, square = joined(
-                stats[row, 0, inner(c)], stats[row, 1, inner(c)], parts[r, 0, inner(c)], parts[r, 1, inner(c)], nk
+                stats[r, 0, inner(c)], stats[r, 1, inner(c)], parts[r, 0, inner(c)], parts[r, 1, inner(c)], nk
             )
             paired[r, 0, inner(c)] = total
             paired[r, 1, inner(c)] = square
-        far_copy(c).start()
+        second_copy(c).start()
 
     def reduce(p):
         c = chunk_at(p)
-        far_copy(c).wait_recv()
-        for r in range(half):
-            row = half * side + r
+        second_copy(c).wait_recv()
+        for r in range(rows):
             total, square = joined(
                 paired[r, 0, inner(c)], paired[r, 1, inner(c)], far[r, 0, inner(c)], far[r, 1, inner(c)], 2 * nk
             )
-            mr[row, 0, inner(c)] = total * (1.0 / count)
-            mr[row, 1, inner(c)] = lax.rsqrt(square * (1.0 / count) + 0.0001)
-        ag_copy(c, mine).start()
+            stat_ref[r, 0, inner(c)] = total * (1.0 / count)
+            stat_ref[r, 1, inner(c)] = lax.rsqrt(square * (1.0 / count) + 0.0001)
 
     def last_position(p, _):
         @pl.when(p < CHUNKS - AHEAD)
@@ -274,7 +264,7 @@
             c = chunk_at(p - END_LAG)
             arrive(final, c)
             update(final, c, True)
-            rs_copy(c).start()
+            first_copy(c).start()
 
         @pl.when((p >= PAIR_LAG) & (p < CHUNKS + PAIR_LAG))
         def _():
@@ -287,13 +277,6 @@
         return 0
 
     lax.fori_loop(0, CHUNKS + FAR_LAG, last_position, 0)
-
-    def finish(c, _):
-        ag_copy(c, other).wait_recv()
-        return 0
-
-    lax.fori_loop(0, CHUNKS, finish, 0)
-    stat_ref[...] = mr[...]
 
     for d in (0, 1):
         pltpu.make_async_copy(dv, dv, lat_send.at[d]).wait()
@@ -302,7 +285,7 @@
         pltpu.make_async_copy(kon.at[:, d], kon.at[:, d], on_send.at[d]).wait()
         whole = te.at[pl.ds(0, STEPS), pl.ds(1, rows), 0]
         pltpu.make_async_copy(whole, whole, lon_send.at[d]).wait()
-    for sem in (rs_send, far_send, ag_send):
+    for sem in (pair_send, far_send):
         pltpu.make_async_copy(parts, far, sem.at[0]).wait()
 
 
@@ -345,16 +328,14 @@
             vmem((STEPS, 2, rows, ni, lanes), F32),
             vmem((STEPS, 2, ni, lanes), F32),
             vmem((rows, 2, ni, lanes), F32),
-            vmem((rows // 2, 2, ni, lanes), F32),
-            vmem((rows // 2, 2, ni, lanes), F32),
-            vmem((rows // 2, 2, ni, lanes), F32),
+            vmem((rows, 2, ni, lanes), F32),
+            vmem((rows, 2, ni, lanes), F32),
             vmem((rows, 2, ni, lanes), F32),
             dma((3,)),
             dma((2,)), dma((2, STEPS, CHUNKS)),
             dma((2,)), dma((2, STEPS)),
             dma((2,)), dma((2, STEPS, CHUNKS)),
             dma((2,)), dma((2, STEPS, CHUNKS)),
-            dma((1,)), dma((CHUNKS,)),
             dma((1,)), dma((CHUNKS,)),
             dma((1,)), dma((CHUNKS,)),
         ],

time: 163 us -> 163 us (level); the launches traced: 163 us -> 161 us
  Pallas kernels: 162 us -> 160 us
    pallas_call x1, Pallas kernels: 159 us -> 157 us  [on_device(): pl.pallas_call(functools.partial(stencil_kernel, n_lat, n_lon, n_lev), ou...]
where the time goes in v3:
time: 163 us; the launch traced here: 161 us
  Pallas kernels  160 us (98%)
    pallas_call x1, Pallas kernels, on_device(): pl.pallas_call(functools.partial(stencil_kernel, n_lat, n_lon, n_lev), ou...  157 us
    pallas_call x1, Pallas kernels, on_device(): pl.pallas_call(scale_kernel, out_shape=(whole, whole), in_specs=[in_vmem,...  3.34 us

profile of v3, /device:TPU:56, one launch (start us, length us, event | category | flops | bytes accessed | tf_op | source)
XLA Modules:
  0.0 160.8 jit_solution(17990140001849803052)
XLA Ops:
  0.6 156.8 %stencil.1 = (f32[4,128,16,128]{3,2,1,0:T(8,128)S(1)}, f32[4,2,128,128]{3,2,1,0:T(8,128)S(1)}) custom-call(f32[4,128,16,128]{3,2,1,0:T(8,128)} %t_hbm.1, f32[4,128,16,128]{3,2,1,0:T(8,128)} %d_hbm.1, f32[4,128,16,128]{3,2,1,0:T(8,128)} %s_hbm.1), custom_call_target="tpu_custom_call" | custom-call | tf_op jit(solution)/shard_map/stencil/pallas_call | solution.py:318
  157.4 3.3 %scale.1 = (f32[4,128,16,128]{3,2,1,0:T(8,128)}, f32[4,128,16,128]{3,2,1,0:T(8,128)}) custom-call(f32[4,128,16,128]{3,2,1,0:T(8,128)S(1)} %get-tuple-element.4.t_ref, f32[4,2,128,128]{3,2,1,0:T(8,128)S(1)} %get-tuple-element.5.m_ref), custom_call_target="tpu_custom_call" | custom-call | tf_op jit(solution)/shard_map/scale/pallas_call | solution.py:348
